TPU v7x, 32 devices: a whole 2x2x4 slice. The times are simulated.
32 devices in a mesh: grp: 2 (over y), row: 16 (over z, x, core).
Axes of the slice: x: 2, y: 2, z: 4, core: 2. Of those that a mesh axis runs over, the one named last changes fastest.
Arguments:
- cells: float32 [256, 128, 192], P(('grp', 'row')), parts along dimension 0, may hold values from -6 to 6
- n_train: int32 [2], P('grp'), parts along dimension 0, may hold values from 16 to 127
- present: int32 [256], P('grp'), parts along dimension 0, may hold values from 0 to 1, as said below
- norm_gain: float32 [3, 192], replicated, may hold values from 0.1 to 1.9
- feat_qkv: bfloat16 [3, 192, 192], replicated, may hold values from -6 to 6
- feat_out: bfloat16 [192, 192], replicated, may hold values from -0.4375 to 0.4375
- item_qkv: bfloat16 [3, 192, 192], replicated, may hold values from -6 to 6
- item_out: bfloat16 [192, 192], replicated, may hold values from -0.875 to 0.875
- mlp_in: bfloat16 [192, 768], replicated, may hold values from -0.4375 to 0.4375
- mlp_out: bfloat16 [768, 192], replicated, may hold values from -0.21875 to 0.21875
Outputs:
- result: float32 [256, 128, 192], P(('grp', 'row')), parts along dimension 0
There are 2 independent parts, one for each index of `grp`. A program takes and returns all parts, laid end to end along the dimension named above; an argument that names none is the same for every part. Nothing has to cross between parts.
Inputs may be any that keep to these rules, and one draw needn't show every extreme that they name: At least one of the 128 features is present.
All inputs are finite; a program needn't handle non-finite values.
Results may differ from a plain program's by a relative error of at most 0.03.
The roundings to bfloat16 on the way count: a program that leaves them out, or rounds other values in their place, can miss the bound.
Values may be sent and summed in bfloat16 or wider, within the bound.
A program may use at most 64 MiB of HBM per device.

v0:
```python
import functools
import math

import jax
import jax.numpy as jnp
from jax import lax
from jax.experimental import pallas as pl
from jax.experimental.pallas import tpu as pltpu
from jax.sharding import PartitionSpec as P

HEADS = 6
LANES = 128
SUBLANES = 8


norm_floor = 0.25
masked_score = -1e30


def layer_norm(stream, gain):
    average = jnp.mean(stream, axis=-1, keepdims=True)
    centred = stream - average
    spread = jnp.mean(centred * centred, axis=-1, keepdims=True)
    return centred * lax.rsqrt(spread + norm_floor) * gain


def softmax_rows(scores):
    largest = jnp.max(scores, axis=-1, keepdims=True)
    exponent = jnp.exp(scores - largest)
    return exponent / jnp.sum(exponent, axis=-1, keepdims=True)


def plain_body(
    cells, n_train, present, norm_gain, feat_qkv, feat_out, item_qkv, item_out, mlp_in, mlp_out
):
    row_dev, feature_count, model_width = cells.shape
    devices_row = lax.axis_size("row")
    total_rows = row_dev * devices_row
    feat_dev = feature_count // devices_row
    head_size = model_width // HEADS
    scale = 1.0 / math.sqrt(head_size)
    query_rows = min(512, total_rows)
    highest = lax.Precision.HIGHEST
    normed = layer_norm(cells, norm_gain[0]).astype(jnp.bfloat16)
    triplet = jnp.einsum("rfe,ced->crfd", normed, feat_qkv, preferred_element_type=jnp.float32)
    triplet = triplet.reshape(3, row_dev, feature_count, HEADS, head_size)
    feat_values = triplet[2].astype(jnp.bfloat16)
    scores = jnp.einsum("rfhd,rghd->rhfg", triplet[0], triplet[1], precision=highest) * scale
    scores = jnp.where(present[None, None, None, :] > 0, scores, masked_score)
    weights = softmax_rows(scores).astype(jnp.bfloat16)
    context = jnp.einsum(
        "rhfg,rghd->rfhd", weights, feat_values, preferred_element_type=jnp.float32
    ).astype(jnp.bfloat16)
    context = context.reshape(row_dev, feature_count, model_width)
    cells_mid = cells + jnp.dot(context, feat_out, preferred_element_type=jnp.float32)
    key_live = lax.iota(jnp.int32, total_rows) < n_train[0]
    arrived = lax.all_to_all(
        cells_mid.reshape(row_dev, devices_row, feat_dev, model_width).astype(jnp.bfloat16),
        "row",
        split_axis=1,
        concat_axis=0,
        tiled=True,
    ).astype(jnp.float32)
    members = arrived.shape[2]
    stream = arrived.reshape(total_rows, members, model_width)
    normed_rows = layer_norm(stream, norm_gain[1]).astype(jnp.bfloat16)
    triples = jnp.einsum("rke,ced->kcrd", normed_rows, item_qkv, preferred_element_type=jnp.float32)

    def one_feature(triple):
        keys = triple[1].reshape(total_rows, HEADS, head_size)
        values = triple[2].astype(jnp.bfloat16).reshape(total_rows, HEADS, head_size)
        queries = triple[0].reshape(total_rows // query_rows, query_rows, HEADS, head_size)

        def query_group(chosen):
            group_scores = jnp.einsum("qhd,shd->hqs", chosen, keys, precision=highest) * scale
            group_scores = jnp.where(key_live[None, None, :], group_scores, masked_score)
            group_weights = softmax_rows(group_scores).astype(jnp.bfloat16)
            return jnp.einsum(
                "hqs,shd->qhd", group_weights, values, preferred_element_type=jnp.float32
            ).astype(jnp.bfloat16)

        return lax.map(query_group, queries).reshape(total_rows, model_width)

    gathered = lax.map(one_feature, triples)
    late = stream + jnp.dot(
        jnp.transpose(gathered, (1, 0, 2)), item_out, preferred_element_type=jnp.float32
    )
    normed_late = layer_norm(late, norm_gain[2]).astype(jnp.bfloat16)
    hidden = jax.nn.gelu(
        jnp.dot(normed_late, mlp_in, preferred_element_type=jnp.float32), approximate=False
    ).astype(jnp.bfloat16)
    updated = late + jnp.dot(hidden, mlp_out, preferred_element_type=jnp.float32)
    returned = lax.all_to_all(
        updated.reshape(total_rows, 1, members, model_width).astype(jnp.bfloat16),
        "row",
        split_axis=0,
        concat_axis=1,
        tiled=True,
    ).astype(jnp.float32)
    return returned.reshape(row_dev, feature_count, model_width)


def matmul(left, right, dims=(1, 0)):
    return lax.dot_general(
        left, right, (((dims[0],), (dims[1],)), ((), ())), preferred_element_type=jnp.float32
    )


def identity(size):
    down = lax.broadcasted_iota(jnp.int32, (size, size), 0)
    across = lax.broadcasted_iota(jnp.int32, (size, size), 1)
    return jnp.where(down == across, 1.0, 0.0).astype(jnp.bfloat16)


def prepare_weights(qkv_ref, turned_ref, spread_ref):
    width = qkv_ref.shape[1]
    head = width // HEADS
    eye = identity(width)
    turned_ref[:width, :] = matmul(eye, qkv_ref[0], (1, 1)).astype(jnp.bfloat16)
    turned_ref[width:, :] = matmul(eye, qkv_ref[2], (1, 1)).astype(jnp.bfloat16)
    down = lax.broadcasted_iota(jnp.int32, (width, 4 * width), 0)
    across = lax.broadcasted_iota(jnp.int32, (width, 4 * width), 1)
    source = (across // (4 * head)) * head + across % head
    pick = jnp.where(down == source, 1.0, 0.0).astype(jnp.bfloat16)
    spread_ref[...] = matmul(qkv_ref[1], pick).astype(jnp.bfloat16)


def attention(normed, turned_ref, spread_ref, bias_ref):
    tokens, width = normed.shape
    size = bias_ref.shape[0]
    head = width // HEADS
    wide = 4 * head
    turned = matmul(turned_ref[...], normed, (1, 1))
    keys = matmul(normed, spread_ref[...])
    queries = turned[:width] * (math.log2(math.e) / math.sqrt(head))
    query_high = queries.astype(jnp.bfloat16)
    query_low = (queries - query_high.astype(jnp.float32)).astype(jnp.bfloat16)
    values = turned[width:].astype(jnp.bfloat16)
    lane = lax.broadcasted_iota(jnp.int32, (1, 4 * width), 1)
    rounded = keys.astype(jnp.bfloat16).astype(jnp.float32)
    keys = jnp.where(lane % wide < 2 * head, keys, keys - rounded).astype(jnp.bfloat16)
    blocks = []
    for block in range(tokens // size):
        here = slice(block * size, (block + 1) * size)
        contexts = []
        for h in range(HEADS):
            rows = slice(h * head, (h + 1) * head)
            high, low = query_high[rows, here], query_low[rows, here]
            query = jnp.concatenate([high, low, high, low], axis=0)
            scores = matmul(keys[here, h * wide : (h + 1) * wide], query) + bias_ref[...]
            exponent = jnp.exp2(scores - jnp.max(scores, axis=0, keepdims=True))
            share = 1.0 / jnp.sum(exponent, axis=0, keepdims=True)
            weights = (exponent * share).astype(jnp.bfloat16)
            contexts.append(matmul(values[rows, here], weights))
        blocks.append(jnp.concatenate(contexts, axis=0))
    return blocks


def kernel(
    devices,
    n_train_ref, cells_ref, present_ref, gain_ref, feat_qkv_ref, feat_out_ref, item_qkv_ref,
    item_out_ref, mlp_in_ref, mlp_out_ref,
    out_ref,
    turned_f, spread_f, turned_i, spread_i, bias_f, bias_i, mid_a, mid_b, mid, send, recv, back,
    home, send_sem, recv_sem, back_sem, home_sem,
):
    me = lax.axis_index("row")
    rows, feats, width = cells_ref.shape
    feat_dev = feats // devices
    pairs = feat_dev // 2
    total_rows = rows * devices
    block = 2 * rows
    group = devices * block
    rest = width - LANES
    order = range(1, devices)

    def pack(slots, pair, tokens):
        last = tokens[:, LANES:].reshape(devices, 2, rows, rest)
        last = jnp.concatenate([last[:, 0], last[:, 1]], axis=-1)
        slots[pair, :, :block] = tokens[:, :LANES].reshape(devices, block, LANES).astype(jnp.bfloat16)
        slots[pair, :, block:] = last.astype(jnp.bfloat16)

    def unpack(slots, pair):
        first = slots[pair, :, :block].astype(jnp.float32).reshape(devices, 2, rows, LANES)
        last = slots[pair, :, block:].astype(jnp.float32)
        last = jnp.concatenate(
            [last[:, None, :, one * rest : (one + 1) * rest] for one in range(2)], axis=1
        )
        return jnp.concatenate([first, last], axis=-1)

    barrier = pltpu.get_barrier_semaphore()

    def greet(step, carry):
        pl.semaphore_signal(
            barrier, inc=1, device_id={"row": lax.rem(me + step, devices)},
            device_id_type=pl.DeviceIdType.MESH,
        )
        return carry

    lax.fori_loop(1, devices, greet, 0)

    prepare_weights(feat_qkv_ref, turned_f, spread_f)
    live = jnp.where(present_ref[...] > 0, 0.0, masked_score)
    bias_f[...] = jnp.broadcast_to(live, (feats, feats)).T
    def feature_rows(step, carry):
        cells = cells_ref[pl.ds(step * 2, 2)].reshape(2 * feats, width)
        normed = layer_norm(cells, gain_ref[0:1, :]).astype(jnp.bfloat16)
        contexts = attention(normed, turned_f, spread_f, bias_f)
        context = jnp.concatenate(contexts, axis=1).astype(jnp.bfloat16)
        updated = cells + matmul(context, feat_out_ref[...], (0, 0))
        here = pl.ds(pl.multiple_of(step * 2 * feats, 2 * feats), 2 * feats)
        mid_a[here, :] = updated[:, :LANES]
        mid_b[here, :rest] = updated[:, LANES:]
        return carry

    lax.fori_loop(0, rows // 2, feature_rows, 0, unroll=2)

    def outgoing(pair, step):
        to = lax.rem(me + step, devices)
        return pltpu.make_async_remote_copy(
            src_ref=send.at[pair, to], dst_ref=recv.at[pair, me],
            send_sem=send_sem.at[pair, step], recv_sem=recv_sem.at[pair, step],
            device_id={"row": to}, device_id_type=pl.DeviceIdType.MESH,
        )

    def returning(pair, step):
        to = lax.rem(me + step, devices)
        return pltpu.make_async_remote_copy(
            src_ref=back.at[pair, to], dst_ref=home.at[pair, me],
            send_sem=back_sem.at[pair, step], recv_sem=home_sem.at[pair, step],
            device_id={"row": to}, device_id_type=pl.DeviceIdType.MESH,
        )

    def each(act):
        def one(step, carry):
            act(step)
            return carry

        lax.fori_loop(1, devices, one, 0)

    pl.semaphore_wait(barrier, devices - 1)

    for pair in range(pairs):
        firsts, lasts = [], []
        for owner in range(devices):
            for one in range(2):
                take = pl.ds(owner * feat_dev + pair * 2 + one, rows, stride=feats)
                firsts.append(mid_a[take, :])
                lasts.append(mid_b[take, :])
        stream = jnp.concatenate(
            [jnp.concatenate(firsts, axis=0), jnp.concatenate(lasts, axis=0)[:, :rest]], axis=1
        )
        mid[pair] = stream
        normed = layer_norm(stream, gain_ref[1:2, :])
        pack(send, pair, normed)
        recv[pair, me] = send[pair, me]
        for step in order:
            outgoing(pair, step).start()

    prepare_weights(item_qkv_ref, turned_i, spread_i)
    number = lax.broadcasted_iota(jnp.int32, (total_rows, total_rows), 0)
    bias_i[...] = jnp.where(number < n_train_ref[0], 0.0, masked_score)

    def item_pair(pair, carry):
        each(lambda step: outgoing(pair, step).wait_recv())
        arrived = unpack(recv, pair)
        normed = jnp.concatenate(
            [arrived[:, one].reshape(total_rows, width) for one in range(2)], axis=0
        ).astype(jnp.bfloat16)
        contexts = attention(normed, turned_i, spread_i, bias_i)
        first = jnp.concatenate(
            [c[:LANES].T.reshape(devices, 1, rows, LANES) for c in contexts], axis=1
        )
        last = jnp.concatenate([c[LANES:] for c in contexts], axis=0).T
        back[pair, :, :block] = first.reshape(devices, block, LANES).astype(jnp.bfloat16)
        back[pair, :, block:] = last.reshape(devices, rows, LANES).astype(jnp.bfloat16)
        home[pair, me] = back[pair, me]
        for step in order:
            returning(pair, step).start()
        each(lambda step: outgoing(pair, step).wait_send())
        return carry

    lax.fori_loop(0, pairs, item_pair, 0)

    def finish(pair, carry):
        each(lambda step: returning(pair, step).wait_send())
        each(lambda step: returning(pair, step).wait_recv())
        context = unpack(home, pair).reshape(group, width).astype(jnp.bfloat16)
        late = mid[pair] + matmul(context, item_out_ref[...])
        normed = layer_norm(late, gain_ref[2:3, :]).astype(jnp.bfloat16)
        inner = matmul(normed, mlp_in_ref[...])
        hidden = (0.5 * inner * (1.0 + lax.erf(inner * math.sqrt(0.5)))).astype(jnp.bfloat16)
        done = late + matmul(hidden, mlp_out_ref[...], (1, 1))
        for owner in range(devices):
            for one in range(2):
                start = (owner * 2 + one) * rows
                put = pl.ds(owner * feat_dev + pair * 2 + one, rows, stride=feats)
                mid_a[put, :] = done[start : start + rows, :LANES]
                mid_b[put, :rest] = done[start : start + rows, LANES:]
        return carry

    lax.fori_loop(0, pairs, finish, 0)
    for row in range(rows):
        out_ref[row, :, :LANES] = mid_a[row * feats : (row + 1) * feats, :]
        out_ref[row, :, LANES:] = mid_b[row * feats : (row + 1) * feats, :rest]


def body(
    cells, n_train, present, norm_gain, feat_qkv, feat_out, item_qkv, item_out, mlp_in, mlp_out
):
    devices = lax.axis_size("row")
    rows, feats, width = cells.shape
    feat_dev = feats // devices
    fits = rows == SUBLANES and feat_dev % 2 == 0 and 2 * width == 3 * LANES
    fits = fits and rows * devices == LANES and feats == LANES and width % (HEADS * 16) == 0
    if not fits:
        return plain_body(
            cells, n_train, present, norm_gain, feat_qkv, feat_out, item_qkv, item_out, mlp_in,
            mlp_out,
        )
    total_rows = rows * devices
    pairs = feat_dev // 2
    vmem = pl.BlockSpec(memory_space=pltpu.VMEM)
    bf16, f32 = jnp.bfloat16, jnp.float32
    slots = pltpu.VMEM((pairs, devices, 3 * rows, LANES), bf16)
    sems = pltpu.SemaphoreType.DMA((pairs, devices))
    return pl.pallas_call(
        functools.partial(kernel, devices),
        out_shape=jax.ShapeDtypeStruct(cells.shape, f32),
        in_specs=[pl.BlockSpec(memory_space=pltpu.SMEM)] + [vmem] * 9,
        out_specs=vmem,
        scratch_shapes=[
            pltpu.VMEM((2 * width, width), bf16),
            pltpu.VMEM((width, 4 * width), bf16),
            pltpu.VMEM((2 * width, width), bf16),
            pltpu.VMEM((width, 4 * width), bf16),
            pltpu.VMEM((feats, feats), f32),
            pltpu.VMEM((total_rows, total_rows), f32),
            pltpu.VMEM((rows * feats, LANES), f32),
            pltpu.VMEM((rows * feats, LANES), f32),
            pltpu.VMEM((pairs, 2 * total_rows, width), f32),
            slots, slots, slots, slots, sems, sems, sems, sems,
        ],
        compiler_params=pltpu.CompilerParams(
            collective_id=0, has_side_effects=True, vmem_limit_bytes=48 * 1024 * 1024
        ),
    )(
        n_train, cells, present.reshape(1, feats), norm_gain, feat_qkv, feat_out, item_qkv, item_out,
        mlp_in, mlp_out.T,
    )


def solution(mesh):
    return jax.shard_map(
        body,
        mesh=mesh,
        in_specs=(
            P(("grp", "row"), None, None),
            P("grp"),
            P("grp"),
            P(),
            P(),
            P(),
            P(),
            P(),
            P(),
            P(),
        ),
        out_specs=P(("grp", "row"), None, None),
        check_vma=False,
    )
```

profile of v0, /device:TPU:0, one launch (start us, length us, event | category | flops | bytes accessed | tf_op | source)
XLA Modules:
  0.0 35.0 jit_solution(9610561558701363064)
XLA Ops:
  0.7 0.0 copy-start
  0.7 0.0 copy-start.1
  0.7 0.0 copy-start.2
  0.7 0.0 copy-start.3
  0.7 0.0 copy-start.4
  0.7 0.0 copy-start.5
  0.7 0.0 copy-start.6
  0.7 0.0 copy-start.7
  0.7 1.6 %copy.11.cells_ref = f32[8,128,192]{2,1,0:T(8,128)S(1)} copy(f32[8,128,192]{1,2,0:T(8,128)} %param.10) | data formatting | bytes 1572864 | tf_op args[0]
  2.3 0.0 copy-done
  2.3 0.0 copy-done.1
  2.3 0.0 copy-done.2
  2.3 0.0 copy-done.3
  2.3 0.0 copy-done.4
  2.3 0.0 copy-done.5
  2.4 0.0 copy-done.6
  2.4 0.0 copy-done.7
  2.4 31.4 %shard_map.100 = f32[8,128,192]{2,1,0:T(8,128)S(1)} custom-call(s32[1]{0:T(128)S(6)} %copy.13.n_train_ref, f32[8,128,192]{2,1,0:T(8,128)S(1)} %copy.11.cells_ref, s32[1,128]{1,0:T(1,128)S(1)} %bitcast.3, f32[3,192]{1,0:T(4,128)S(1)} %copy-done.6, bf16[3,192,192]{2,1,0:T(8,128)(2,1)S(1)} %copy-done, bf16[192,192]{1,0:T(8,128)(2,1)S(1)} %copy-done.4, ...), custom_call_target="tpu_custom_call" | custom-call | tf_op jit(solution)/shard_map/pallas_call | solution.py:327
  33.8 1.2 %copy.12 = f32[8,128,192]{1,2,0:T(8,128)} copy(f32[8,128,192]{2,1,0:T(8,128)S(1)} %shard_map.100) | data formatting | bytes 1572864 | tf_op jit(solution)/shard_map/pallas_call | solution.py:327
Async XLA Ops:
  0.7 1.6 %copy-start = (bf16[3,192,192]{2,1,0:T(8,128)(2,1)S(1)}, bf16[3,192,192]{2,1,0:T(8,128)(2,1)}, u32[]{:S(2)}) copy-start(bf16[3,192,192]{2,1,0:T(8,128)(2,1)} %feat_qkv_ref.1) | copy-start | bytes 663556
  0.7 1.6 %copy-start.1 = (bf16[3,192,192]{2,1,0:T(8,128)(2,1)S(1)}, bf16[3,192,192]{2,1,0:T(8,128)(2,1)}, u32[]{:S(2)}) copy-start(bf16[3,192,192]{2,1,0:T(8,128)(2,1)} %item_qkv_ref.1) | copy-start | bytes 663556
  0.7 1.6 %copy-start.2 = (bf16[192,768]{1,0:T(8,128)(2,1)S(1)}, bf16[192,768]{1,0:T(8,128)(2,1)}, u32[]{:S(2)}) copy-start(bf16[192,768]{1,0:T(8,128)(2,1)} %mlp_in_ref.1) | copy-start | bytes 884740
  0.7 1.6 %copy-start.3 = (bf16[768,192]{0,1:T(8,128)(2,1)S(1)}, bf16[768,192]{0,1:T(8,128)(2,1)}, u32[]{:S(2)}) copy-start(bf16[768,192]{0,1:T(8,128)(2,1)} %param.19) | copy-start | bytes 884740
  0.7 1.6 %copy-start.4 = (bf16[192,192]{1,0:T(8,128)(2,1)S(1)}, bf16[192,192]{1,0:T(8,128)(2,1)}, u32[]{:S(2)}) copy-start(bf16[192,192]{1,0:T(8,128)(2,1)} %feat_out_ref.1) | copy-start | bytes 221188
  0.7 1.6 %copy-start.5 = (bf16[192,192]{1,0:T(8,128)(2,1)S(1)}, bf16[192,192]{1,0:T(8,128)(2,1)}, u32[]{:S(2)}) copy-start(bf16[192,192]{1,0:T(8,128)(2,1)} %item_out_ref.1) | copy-start | bytes 221188
  0.7 1.6 %copy-start.6 = (f32[3,192]{1,0:T(4,128)S(1)}, f32[3,192]{1,0:T(4,128)}, u32[]{:S(2)}) copy-start(f32[3,192]{1,0:T(4,128)} %gain_ref.1) | copy-start | bytes 6916
  0.7 1.6 %copy-start.7 = (s32[128]{0:T(128)S(1)}, s32[128]{0:T(128)}, u32[]{:S(2)}) copy-start(s32[128]{0:T(128)} %param.12) | copy-start | bytes 1540
where the time goes:
time: 35.2 us; the launch traced here: 35 us
  Pallas kernels  31.4 us (89%)
  local copies, waits for them, and re-layouts  2.81 us (8%)
  between operations  0.79 us (2%)
    pallas_call x1, Pallas kernels, body(): pl.pallas_call(functools.partial(kernel, devices), out_shape=jax.ShapeDty...  31.4 us
    unnamed x17, local copies, waits for them, and re-layouts  1.59 us
    pallas_call x1, local copies, waits for them, and re-layouts, body(): pl.pallas_call(functools.partial(kernel, devices), out_shape=jax.ShapeDty...  1.22 us

commit v1 on v0

v1 whole, which is shorter than its diff:
```python
import functools
import math

import jax
import jax.numpy as jnp
from jax import lax
from jax.experimental import pallas as pl
from jax.experimental.pallas import tpu as pltpu
from jax.sharding import PartitionSpec as P

HEADS = 6
LANES = 128
SUBLANES = 8


norm_floor = 0.25
masked_score = -1e30


def layer_norm(stream, gain):
    average = jnp.mean(stream, axis=-1, keepdims=True)
    centred = stream - average
    spread = jnp.mean(centred * centred, axis=-1, keepdims=True)
    return centred * lax.rsqrt(spread + norm_floor) * gain


def softmax_rows(scores):
    largest = jnp.max(scores, axis=-1, keepdims=True)
    exponent = jnp.exp(scores - largest)
    return exponent / jnp.sum(exponent, axis=-1, keepdims=True)


def plain_body(
    cells, n_train, present, norm_gain, feat_qkv, feat_out, item_qkv, item_out, mlp_in, mlp_out
):
    row_dev, feature_count, model_width = cells.shape
    devices_row = lax.axis_size("row")
    total_rows = row_dev * devices_row
    feat_dev = feature_count // devices_row
    head_size = model_width // HEADS
    scale = 1.0 / math.sqrt(head_size)
    query_rows = min(512, total_rows)
    highest = lax.Precision.HIGHEST
    normed = layer_norm(cells, norm_gain[0]).astype(jnp.bfloat16)
    triplet = jnp.einsum("rfe,ced->crfd", normed, feat_qkv, preferred_element_type=jnp.float32)
    triplet = triplet.reshape(3, row_dev, feature_count, HEADS, head_size)
    feat_values = triplet[2].astype(jnp.bfloat16)
    scores = jnp.einsum("rfhd,rghd->rhfg", triplet[0], triplet[1], precision=highest) * scale
    scores = jnp.where(present[None, None, None, :] > 0, scores, masked_score)
    weights = softmax_rows(scores).astype(jnp.bfloat16)
    context = jnp.einsum(
        "rhfg,rghd->rfhd", weights, feat_values, preferred_element_type=jnp.float32
    ).astype(jnp.bfloat16)
    context = context.reshape(row_dev, feature_count, model_width)
    cells_mid = cells + jnp.dot(context, feat_out, preferred_element_type=jnp.float32)
    key_live = lax.iota(jnp.int32, total_rows) < n_train[0]
    arrived = lax.all_to_all(
        cells_mid.reshape(row_dev, devices_row, feat_dev, model_width).astype(jnp.bfloat16),
        "row",
        split_axis=1,
        concat_axis=0,
        tiled=True,
    ).astype(jnp.float32)
    members = arrived.shape[2]
    stream = arrived.reshape(total_rows, members, model_width)
    normed_rows = layer_norm(stream, norm_gain[1]).astype(jnp.bfloat16)
    triples = jnp.einsum("rke,ced->kcrd", normed_rows, item_qkv, preferred_element_type=jnp.float32)

    def one_feature(triple):
        keys = triple[1].reshape(total_rows, HEADS, head_size)
        values = triple[2].astype(jnp.bfloat16).reshape(total_rows, HEADS, head_size)
        queries = triple[0].reshape(total_rows // query_rows, query_rows, HEADS, head_size)

        def query_group(chosen):
            group_scores = jnp.einsum("qhd,shd->hqs", chosen, keys, precision=highest) * scale
            group_scores = jnp.where(key_live[None, None, :], group_scores, masked_score)
            group_weights = softmax_rows(group_scores).astype(jnp.bfloat16)
            return jnp.einsum(
                "hqs,shd->qhd", group_weights, values, preferred_element_type=jnp.float32
            ).astype(jnp.bfloat16)

        return lax.map(query_group, queries).reshape(total_rows, model_width)

    gathered = lax.map(one_feature, triples)
    late = stream + jnp.dot(
        jnp.transpose(gathered, (1, 0, 2)), item_out, preferred_element_type=jnp.float32
    )
    normed_late = layer_norm(late, norm_gain[2]).astype(jnp.bfloat16)
    hidden = jax.nn.gelu(
        jnp.dot(normed_late, mlp_in, preferred_element_type=jnp.float32), approximate=False
    ).astype(jnp.bfloat16)
    updated = late + jnp.dot(hidden, mlp_out, preferred_element_type=jnp.float32)
    returned = lax.all_to_all(
        updated.reshape(total_rows, 1, members, model_width).astype(jnp.bfloat16),
        "row",
        split_axis=0,
        concat_axis=1,
        tiled=True,
    ).astype(jnp.float32)
    return returned.reshape(row_dev, feature_count, model_width)


def matmul(left, right, dims=(1, 0)):
    return lax.dot_general(
        left, right, (((dims[0],), (dims[1],)), ((), ())), preferred_element_type=jnp.float32
    )


def pick_rows(width, total):
    down = lax.broadcasted_iota(jnp.int32, (width, total), 0)
    across = lax.broadcasted_iota(jnp.int32, (width, total), 1)
    source = jnp.where(across < width, across, across - (total - width))
    return jnp.where(down == source, 1.0, 0.0).astype(jnp.bfloat16)


def turn(weight, total):
    return matmul(weight, pick_rows(weight.shape[0], total), (0, 0)).astype(jnp.bfloat16)


def prepare_weights(qkv_ref, turned_ref, spread_ref):
    width = qkv_ref.shape[1]
    total = turned_ref.shape[1]
    head = width // HEADS
    turned_ref[:width, :] = turn(qkv_ref[0], total)
    turned_ref[width:, :] = turn(qkv_ref[2], total)
    down = lax.broadcasted_iota(jnp.int32, (width, 4 * width), 0)
    across = lax.broadcasted_iota(jnp.int32, (width, 4 * width), 1)
    source = (across // (4 * head)) * head + across % head
    pick = jnp.where(down == source, 1.0, 0.0).astype(jnp.bfloat16)
    spread = matmul(qkv_ref[1], pick).astype(jnp.bfloat16)
    spread_ref[:width, :] = spread
    if total > width:
        spread_ref[width:, :] = spread[2 * width - total :]


def attention(turned, keys, bias_ref):
    width = turned.shape[0] // 2
    tokens = turned.shape[1]
    size = bias_ref.shape[0]
    head = width // HEADS
    wide = 4 * head
    queries = turned[:width] * (math.log2(math.e) / math.sqrt(head))
    query_high = queries.astype(jnp.bfloat16)
    query_low = (queries - query_high.astype(jnp.float32)).astype(jnp.bfloat16)
    values = turned[width:].astype(jnp.bfloat16)
    lane = lax.broadcasted_iota(jnp.int32, (1, 4 * width), 1)
    rounded = keys.astype(jnp.bfloat16).astype(jnp.float32)
    keys = jnp.where(lane % wide < 2 * head, keys, keys - rounded).astype(jnp.bfloat16)
    blocks = []
    for block in range(tokens // size):
        here = slice(block * size, (block + 1) * size)
        contexts = []
        for h in range(HEADS):
            rows = slice(h * head, (h + 1) * head)
            high, low = query_high[rows, here], query_low[rows, here]
            query = jnp.concatenate([high, low, high, low], axis=0)
            scores = matmul(keys[here, h * wide : (h + 1) * wide], query) + bias_ref[...]
            exponent = jnp.exp2(scores - jnp.max(scores, axis=0, keepdims=True))
            share = 1.0 / jnp.sum(exponent, axis=0, keepdims=True)
            weights = (exponent * share).astype(jnp.bfloat16)
            contexts.append(matmul(values[rows, here], weights))
        blocks.append(jnp.concatenate(contexts, axis=0))
    return blocks


def norm_down(stream, gain):
    average = jnp.mean(stream, axis=0, keepdims=True)
    centred = stream - average
    spread = jnp.mean(centred * centred, axis=0, keepdims=True)
    return centred * lax.rsqrt(spread + norm_floor) * gain


def kernel(
    devices,
    n_train_ref, cells_ref, present_hbm, gain_hbm, feat_qkv_hbm, feat_out_hbm, item_qkv_hbm,
    item_out_hbm, mlp_in_hbm, mlp_out_hbm,
    out_ref,
    present_ref, gain_ref, feat_qkv_ref, feat_out_ref, item_qkv_ref, item_out_ref, mlp_in_ref,
    mlp_out_ref, turned_f, spread_f, turned_i, spread_i, out_f, out_i, into, gains, bias_f, bias_i,
    mid, sort_a, sort_b, sort_i, loose_a, loose_b, send, recv, back, home, in_sem, send_sem, recv_sem,
    back_sem, home_sem,
):
    me = lax.axis_index("row")
    rows, width, feats = cells_ref.shape
    steps = rows // 2
    half = rows // 2
    group = feats // 2
    share = group // devices
    total_rows = rows * devices
    rest = width - LANES
    order = range(1, devices)
    others = pl.ds(0, devices - 1)

    barrier = pltpu.get_barrier_semaphore()
    for shift in order:
        pl.semaphore_signal(
            barrier, inc=1, device_id={"row": lax.rem(me + shift, devices)},
            device_id_type=pl.DeviceIdType.MESH,
        )

    moves = [
        (gain_hbm, gain_ref), (present_hbm, present_ref), (feat_qkv_hbm, feat_qkv_ref),
        (cells_ref.at[pl.ds(0, half)], mid.at[pl.ds(0, half)]), (feat_out_hbm, feat_out_ref),
        (cells_ref.at[pl.ds(half, half)], mid.at[pl.ds(half, half)]),
        (item_qkv_hbm, item_qkv_ref), (item_out_hbm, item_out_ref), (mlp_in_hbm, mlp_in_ref),
        (mlp_out_hbm, mlp_out_ref),
    ]
    loads = [
        pltpu.make_async_copy(source, target, in_sem.at[number])
        for number, (source, target) in enumerate(moves)
    ]
    for load in loads:
        load.start()

    def outgoing(part, side, shift, slots):
        to = lax.rem(me + shift, devices)
        return pltpu.make_async_remote_copy(
            src_ref=send.at[part, side, to if slots is None else slots],
            dst_ref=recv.at[part, side, me if slots is None else slots],
            send_sem=send_sem.at[part, side], recv_sem=recv_sem.at[part, side],
            device_id={"row": to}, device_id_type=pl.DeviceIdType.MESH,
        )

    def returning(side, pair, shift, slots):
        to = lax.rem(me + shift, devices)
        return pltpu.make_async_remote_copy(
            src_ref=back.at[side, pair, to if slots is None else slots],
            dst_ref=home.at[side, pair, me if slots is None else slots],
            send_sem=back_sem.at[side, pair], recv_sem=home_sem.at[side, pair],
            device_id={"row": to}, device_id_type=pl.DeviceIdType.MESH,
        )

    def turned_parts(one, two):
        last = jnp.concatenate([one[LANES:], two[LANES:]], axis=0)
        return [part.T for part in (one[:LANES], two[:LANES], last)]

    def keep(tile, one):
        left = lax.broadcasted_iota(jnp.int32, tile.shape, 1) < rest
        return jnp.where(left if one == 0 else jnp.logical_not(left), tile, 0.0)

    for load in loads[:3]:
        load.wait()
    for number in range(3):
        gains[number] = jnp.broadcast_to(gain_ref[number : number + 1, :], (feats, width)).T
    live = jnp.where(present_ref[...] > 0, 0.0, masked_score)
    bias_f[...] = jnp.broadcast_to(live, (feats, feats)).T
    prepare_weights(feat_qkv_ref, turned_f, spread_f)

    def gain_of(number):
        return jnp.concatenate([gains[number], gains[number]], axis=1)

    def feature_rows(step):
        cells = jnp.concatenate([mid[2 * step], mid[2 * step + 1]], axis=1)
        normed = norm_down(cells, gain_of(0)).astype(jnp.bfloat16)
        turned = matmul(turned_f[...], normed)
        keys = matmul(normed, spread_f[...], (0, 0))
        contexts = attention(turned, keys, bias_f)
        context = jnp.concatenate(contexts, axis=1).astype(jnp.bfloat16)
        updated = cells + matmul(out_f[...], context)
        mid[2 * step] = updated[:, :feats]
        mid[2 * step + 1] = updated[:, feats:]
        normed = norm_down(updated, gain_of(1))
        parts = turned_parts(normed[:, :feats], normed[:, feats:])
        part, inner = 2 * step // half, 2 * step % half
        for side in range(2):
            here = slice(side * group, (side + 1) * group)
            for one in range(2):
                sort_a[part, side, pl.ds(inner + one, group, stride=half), :] = parts[one][here]
            sort_b[part, side, pl.ds(inner // 2, group, stride=half // 2), :] = parts[2][here]

    def dispatch(part, side):
        for shift in order:
            outgoing(part, side, shift, None).start()
        recv[part, side, me] = send[part, side, me]

    for part in range(2):
        if part == 0:
            loads[3].wait()
            loads[4].wait()
            out_f[...] = turn(feat_out_ref[...], width)
        else:
            loads[5].wait()
        for step in range(part * steps // 2, (part + 1) * steps // 2):
            feature_rows(step)
        for side in range(2):
            first = sort_a[part, side].reshape(devices, share * half, LANES)
            last = sort_b[part, side].reshape(devices, share * half // 2, LANES)
            send[part, side, :, : share * half] = first.astype(jnp.bfloat16)
            send[part, side, :, share * half :] = last.astype(jnp.bfloat16)
        if part == 0:
            pl.semaphore_wait(barrier, devices - 1)
            dispatch(0, 0)
    dispatch(1, 0)
    dispatch(0, 1)
    dispatch(1, 1)

    for load in loads[6:]:
        load.wait()
    prepare_weights(item_qkv_ref, turned_i, spread_i)
    out_i[...] = turn(item_out_ref[...], out_i.shape[1])
    into[...] = turn(mlp_in_ref[...], width)
    token = lax.broadcasted_iota(jnp.int32, (total_rows, total_rows), 0)
    number = token % devices * rows + token // devices
    bias_i[...] = jnp.where(number < n_train_ref[0], 0.0, masked_score)

    def item_side(side, carry):
        for part in range(2):
            outgoing(part, side, 1, others).wait_recv()
            tiles = recv[part, side].astype(jnp.float32)
            for device in range(devices):
                start = (device * 2 + part) * share * half
                loose_a[start : start + share * half, :] = tiles[device, : share * half]
                for one in range(2):
                    put = pl.ds(start + one, share * half // 2, stride=2)
                    loose_b[put, :] = keep(tiles[device, share * half :], one)

        def collect(feature):
            pieces = []
            for row in range(rows):
                start = (row // half) * share * half + feature * half + row % half
                take = pl.ds(start, devices, stride=2 * share * half)
                pieces.append(jnp.concatenate([loose_a[take, :], loose_b[take, :]], axis=1))
            return jnp.concatenate(pieces, axis=0)

        for pair in range(2):
            normed = jnp.concatenate([collect(2 * pair), collect(2 * pair + 1)], axis=0)
            normed = normed.astype(jnp.bfloat16)
            turned = matmul(turned_i[...], normed, (1, 1))
            keys = matmul(normed, spread_i[...])
            parts = turned_parts(*attention(turned, keys, bias_i))
            for number, part in enumerate(parts):
                sort_i[pair, number] = part
            for device in range(devices):
                take = pl.ds(device, rows, stride=devices)
                tile = jnp.concatenate([sort_i[pair, n, take, :] for n in range(3)], axis=0)
                back[side, pair, device] = tile.astype(jnp.bfloat16)
            for shift in order:
                returning(side, pair, shift, None).start()
            home[side, pair, me] = back[side, pair, me]
        return carry

    lax.fori_loop(0, 2, item_side, 0)

    def finish_side(side):
        for pair in range(2):
            returning(side, pair, 1, others).wait_recv()
            tiles = home[side, pair].astype(jnp.float32)
            for device in range(devices):
                for one in range(2):
                    start = (device * share + 2 * pair + one) * rows
                    loose_a[start : start + rows, :] = tiles[device, one * rows : (one + 1) * rows]
                    loose_b[start : start + rows, :] = keep(tiles[device, 2 * rows :], one)
        here = slice(side * group, (side + 1) * group)
        for first in range(0, rows, 4):
            chosen = range(first, first + 4)
            context = []
            for row in chosen:
                take = pl.ds(row, group, stride=rows)
                context.append(jnp.concatenate([loose_a[take, :], loose_b[take, :]], axis=1))
            context = jnp.concatenate(context, axis=0).astype(jnp.bfloat16)
            stream = jnp.concatenate([mid[row, :, here] for row in chosen], axis=1)
            late = stream + matmul(out_i[...], context, (1, 1))
            normed = norm_down(late, gain_of(2)).astype(jnp.bfloat16)
            inner = matmul(into[...], normed)
            hidden = (0.5 * inner * (1.0 + lax.erf(inner * math.sqrt(0.5)))).astype(jnp.bfloat16)
            done = late + matmul(mlp_out_ref[...], hidden)
            for number, row in enumerate(chosen):
                out_ref[row, :, here] = done[:, number * group : (number + 1) * group]

    for side in range(2):
        finish_side(side)
    for part in range(2):
        for side in range(2):
            outgoing(part, side, 1, others).wait_send()
            returning(part, side, 1, others).wait_send()


def body(
    cells, n_train, present, norm_gain, feat_qkv, feat_out, item_qkv, item_out, mlp_in, mlp_out
):
    devices = lax.axis_size("row")
    rows, feats, width = cells.shape
    feat_dev = feats // devices
    fits = rows == SUBLANES and feat_dev == SUBLANES and 2 * width == 3 * LANES
    fits = fits and rows * devices == LANES and feats == LANES and width % (HEADS * 16) == 0
    if not fits:
        return plain_body(
            cells, n_train, present, norm_gain, feat_qkv, feat_out, item_qkv, item_out, mlp_in,
            mlp_out,
        )
    total_rows = rows * devices
    hidden = mlp_in.shape[1]
    total = 2 * LANES
    vmem = pl.BlockSpec(memory_space=pltpu.VMEM)
    hbm = pl.BlockSpec(memory_space=pltpu.HBM)
    bf16, f32 = jnp.bfloat16, jnp.float32
    slots = pltpu.VMEM((2, 2, devices, 3 * rows, LANES), bf16)
    sems = pltpu.SemaphoreType.DMA((2, 2))
    loose = pltpu.VMEM((rows * feats // 2, LANES), f32)
    arrays = (
        jnp.swapaxes(cells, 1, 2), present.reshape(1, feats), norm_gain, feat_qkv, feat_out,
        item_qkv, item_out, mlp_in, mlp_out.T,
    )
    arrays = [pltpu.with_memory_space_constraint(array, pltpu.HBM) for array in arrays]
    out = pl.pallas_call(
        functools.partial(kernel, devices),
        out_shape=jax.ShapeDtypeStruct((rows, width, feats), f32),
        in_specs=[pl.BlockSpec(memory_space=pltpu.SMEM)] + [hbm] * 9,
        out_specs=vmem,
        scratch_shapes=[
            pltpu.VMEM((1, feats), jnp.int32),
            pltpu.VMEM((3, width), f32),
            pltpu.VMEM((3, width, width), bf16),
            pltpu.VMEM((width, width), bf16),
            pltpu.VMEM((3, width, width), bf16),
            pltpu.VMEM((width, width), bf16),
            pltpu.VMEM((width, hidden), bf16),
            pltpu.VMEM((width, hidden), bf16),
            pltpu.VMEM((2 * width, width), bf16),
            pltpu.VMEM((width, 4 * width), bf16),
            pltpu.VMEM((2 * width, total), bf16),
            pltpu.VMEM((total, 4 * width), bf16),
            pltpu.VMEM((width, width), bf16),
            pltpu.VMEM((width, total), bf16),
            pltpu.VMEM((hidden, width), bf16),
            pltpu.VMEM((3, width, feats), f32),
            pltpu.VMEM((feats, feats), f32),
            pltpu.VMEM((total_rows, total_rows), f32),
            pltpu.VMEM((rows, width, feats), f32),
            pltpu.VMEM((2, 2, rows * feats // 4, LANES), f32),
            pltpu.VMEM((2, 2, rows * feats // 8, LANES), f32),
            pltpu.VMEM((2, 3, total_rows, LANES), f32),
            loose, loose, slots, slots, slots, slots,
            pltpu.SemaphoreType.DMA((10,)),
            sems, sems, sems, sems,
        ],
        compiler_params=pltpu.CompilerParams(
            collective_id=0, has_side_effects=True, vmem_limit_bytes=48 * 1024 * 1024
        ),
    )(n_train, *arrays)
    return jnp.swapaxes(out, 1, 2)


def solution(mesh):
    return jax.shard_map(
        body,
        mesh=mesh,
        in_specs=(
            P(("grp", "row"), None, None),
            P("grp"),
            P("grp"),
            P(),
            P(),
            P(),
            P(),
            P(),
            P(),
            P(),
        ),
        out_specs=P(("grp", "row"), None, None),
        check_vma=False,
    )
```

time: 35.2 us -> 29.4 us (0.84)
  Pallas kernels: 31.4 us -> 27.7 us
  local copies, waits for them, and re-layouts: 2.81 us -> 0.88 us
    pallas_call x1, Pallas kernels: 31.4 us -> 27.7 us  [body(): pl.pallas_call(functools.partial(kernel, devices), out_shape=jax.ShapeDty...]
    pallas_call x1 -> x0, local copies, waits for them, and re-layouts: 1.22 us -> none  [body(): pl.pallas_call(functools.partial(kernel, devices), out_shape=jax.ShapeDty...]
    unnamed x17 -> x1, local copies, waits for them, and re-layouts: 1.59 us -> 0.88 us
where the time goes in v1:
time: 29.4 us; the launch traced here: 29.2 us
  Pallas kernels  27.7 us (94%)
  local copies, waits for them, and re-layouts  0.88 us (3%)
  between operations  0.66 us (2%)
    pallas_call x1, Pallas kernels, body(): pl.pallas_call(functools.partial(kernel, devices), out_shape=jax.ShapeDty...  27.7 us
    unnamed x1, local copies, waits for them, and re-layouts  0.88 us

profile of v1, /device:TPU:0, one launch (start us, length us, event | category | flops | bytes accessed | tf_op | source)
XLA Modules:
  0.0 29.2 jit_solution(10659183034590183894)
XLA Ops:
  0.7 27.7 %shard_map.100 = f32[8,192,128]{2,1,0:T(8,128)S(1)} custom-call(s32[1]{0:T(128)S(6)} %copy.12.n_train_ref, f32[8,192,128]{2,1,0:T(8,128)} %bitcast.5, s32[1,128]{1,0:T(1,128)} %bitcast.7, f32[3,192]{1,0:T(4,128)} %gain_hbm.1, bf16[3,192,192]{2,1,0:T(8,128)(2,1)} %feat_qkv_hbm.1, bf16[192,192]{1,0:T(8,128)(2,1)} %feat_out_hbm.1, ...), custom_call_target="tpu_custom_call" | custom-call | tf_op jit(solution)/shard_map/pallas_call | solution.py:405
  28.4 0.9 %copy.13 = f32[8,128,192]{1,2,0:T(8,128)} copy(f32[8,128,192]{1,2,0:T(8,128)S(1)} %bitcast.4) | data formatting | bytes 1572864
